TPU v7x, 32 devices: a whole 2x2x4 slice. The times are simulated.
32 devices in a mesh: ctx: 8 (over y, x, core), head: 4 (over z).
Axes of the slice: x: 2, y: 2, z: 4, core: 2. Of those that a mesh axis runs over, the one named last changes fastest.
Arguments:
- q_latent: bfloat16 [2048, 1536], P('ctx', 'head'), may hold values from -70 to 70
- kv_latent: bfloat16 [2048, 576], P('ctx', 'head'), may hold values from -6 to 6
- w_query: bfloat16 [1536, 12288], P(None, 'head'), may hold values from -0.15625 to 0.15625
- w_key: bfloat16 [512, 8192], P(None, 'head'), may hold values from -0.25 to 0.25
- w_value: bfloat16 [512, 8192], P(None, 'head'), may hold values from -0.25 to 0.25
- d_out: bfloat16 [2048, 8192], P('ctx', 'head'), may hold values from -6 to 6
Outputs:
- attn_out: bfloat16 [2048, 8192], P('ctx', 'head')
- grad_qlat: float32 [2048, 1536], P('ctx', 'head')
- grad_kvlat: float32 [2048, 576], P('ctx', 'head')
All inputs are finite; a program needn't handle non-finite values.
Results may differ from a plain program's by a relative error of at most 0.023.
The roundings to bfloat16 on the way count: a program that leaves them out, or rounds other values in their place, can miss the bound.
Values may be sent and summed in bfloat16 or wider, within the bound.
A program may use at most 128 MiB of HBM per device.

v0:
```python
import jax
import jax.numpy as jnp
from jax import lax
from jax.sharding import PartitionSpec as P

KVL = 512
ROPE = 64
NOPE = 128
VDIM = 128
HEAD_DEV = 16


def from_behind(array, axis, by):
    peers = lax.axis_size(axis)
    pairs = [(i, i + by) for i in range(peers) if 0 <= i + by < peers]
    return lax.ppermute(array, axis, pairs)


def on_device(q_latent, kv_latent, w_query, w_key, w_value, d_out):
    block_rows = q_latent.shape[0]
    per_dev = HEAD_DEV
    width = NOPE + ROPE
    softmax_scale = width ** (-0.5)
    queries = jnp.dot(
        lax.all_gather(q_latent, "head", axis=1, tiled=True),
        w_query,
        preferred_element_type=jnp.float32,
    )
    queries = queries.astype(jnp.bfloat16).reshape(block_rows, per_dev, width)
    latent = lax.all_gather(kv_latent, "head", axis=1, tiled=True)

    def expand(latent_rows):
        main_cols = latent_rows[:, :KVL]
        keys_nope = jnp.dot(main_cols, w_key, preferred_element_type=jnp.float32).astype(
            jnp.bfloat16
        )
        values = jnp.dot(main_cols, w_value, preferred_element_type=jnp.float32).astype(
            jnp.bfloat16
        )
        return (
            keys_nope.reshape(block_rows, per_dev, NOPE),
            latent_rows[:, KVL:],
            values.reshape(block_rows, per_dev, VDIM),
        )

    own_keys = expand(latent)
    previous = expand(from_behind(latent, "ctx", 1))
    keys_all = jnp.concatenate([previous[0], own_keys[0]], 0)
    rope_all = jnp.concatenate([previous[1], own_keys[1]], 0)
    values_all = jnp.concatenate([previous[2], own_keys[2]], 0)
    leading = lax.axis_index("ctx") == 0
    query_pos = jnp.arange(block_rows)[:, None]
    key_pos = jnp.arange(2 * block_rows)[None, :]
    visible = jnp.where(
        key_pos < block_rows, jnp.logical_not(leading), key_pos - block_rows <= query_pos
    )[None]
    query_nope = queries[..., :NOPE]
    query_rope = queries[..., NOPE:]
    scores = jnp.einsum("qhd,khd->hqk", query_nope, keys_all, preferred_element_type=jnp.float32)
    scores = (
        scores + jnp.einsum("qhr,kr->hqk", query_rope, rope_all, preferred_element_type=jnp.float32)
    ) * softmax_scale
    scores = jnp.where(visible, scores, jnp.float32(-1e30))
    maxima = jnp.max(scores, -1, keepdims=True)
    expons = jnp.where(visible, jnp.exp(scores - maxima), jnp.float32(0.0))
    probs = expons / jnp.sum(expons, -1, keepdims=True)
    probs_b = probs.astype(jnp.bfloat16)
    output = jnp.einsum(
        "hqk,khd->qhd", probs_b, values_all, preferred_element_type=jnp.float32
    ).astype(jnp.bfloat16)
    grad_out = d_out.reshape(block_rows, per_dev, VDIM)
    dprob = jnp.einsum("qhd,khd->hqk", grad_out, values_all, preferred_element_type=jnp.float32)
    row_dot = jnp.sum(grad_out.astype(jnp.float32) * output.astype(jnp.float32), -1).T[..., None]
    dscore = (probs * (dprob - row_dot) * softmax_scale).astype(jnp.bfloat16)
    grad_qnope = jnp.einsum("hqk,khd->qhd", dscore, keys_all, preferred_element_type=jnp.float32)
    grad_qrope = jnp.einsum("hqk,kr->qhr", dscore, rope_all, preferred_element_type=jnp.float32)
    grad_query = (
        jnp.concatenate([grad_qnope, grad_qrope], -1)
        .astype(jnp.bfloat16)
        .reshape(block_rows, per_dev * width)
    )
    grad_qpart = jnp.dot(grad_query, w_query.T, preferred_element_type=jnp.float32)
    grad_knope = jnp.einsum(
        "hqk,qhd->khd", dscore, query_nope, preferred_element_type=jnp.float32
    ).astype(jnp.bfloat16)
    grad_krope = jnp.einsum(
        "hqk,qhr->khr", dscore, query_rope, preferred_element_type=jnp.float32
    ).astype(jnp.bfloat16)
    grad_value = jnp.einsum(
        "hqk,qhd->khd", probs_b, grad_out, preferred_element_type=jnp.float32
    ).astype(jnp.bfloat16)

    def project(knope_part, krope_part, value_part):
        main_cols = jnp.dot(
            knope_part.reshape(block_rows, per_dev * NOPE),
            w_key.T,
            preferred_element_type=jnp.float32,
        )
        main_cols = main_cols + jnp.dot(
            value_part.reshape(block_rows, per_dev * VDIM),
            w_value.T,
            preferred_element_type=jnp.float32,
        )
        rope_cols = jnp.sum(krope_part.astype(jnp.float32), axis=1)
        return jnp.concatenate([main_cols, rope_cols], -1)

    own_part = project(grad_knope[block_rows:], grad_krope[block_rows:], grad_value[block_rows:])
    earlier = project(grad_knope[:block_rows], grad_krope[:block_rows], grad_value[:block_rows])
    grad_kvpart = own_part + from_behind(earlier.astype(jnp.bfloat16), "ctx", -1).astype(
        earlier.dtype
    )
    grad_qlat, grad_kvlat = (
        lax.psum_scatter(grad_qpart, "head", scatter_dimension=1, tiled=True),
        lax.psum_scatter(grad_kvpart, "head", scatter_dimension=1, tiled=True),
    )
    return (output.reshape(block_rows, per_dev * VDIM), grad_qlat, grad_kvlat)


def solution(mesh):
    return jax.shard_map(
        on_device,
        mesh=mesh,
        in_specs=(
            P("ctx", "head"),
            P("ctx", "head"),
            P(None, "head"),
            P(None, "head"),
            P(None, "head"),
            P("ctx", "head"),
        ),
        out_specs=(P("ctx", "head"), P("ctx", "head"), P("ctx", "head")),
        check_vma=False,
    )
```

profile of v0, /device:TPU:0, one launch (start us, length us, event | category | flops | bytes accessed | tf_op | source)
XLA Modules:
  0.0 189.1 jit_solution(5349100622864666267)
XLA Ops:
  7.2 16.0 %all_gather.6 = bf16[256,576]{0,1:T(8,128)(2,1)S(1)} all-gather(bf16[256,144]{0,1:T(8,128)(2,1)} %param.7), channel_id=1, replica_groups=mesh['ctx'=8,'head'=4] {'head'}, dimensions={1}, use_global_device_ids=true | all-gather | bytes 368640 | tf_op jit(solution)/shard_map/all_gather | solution.py:30
  23.2 2.0 %collective-permute-start = (bf16[256,576]{0,1:T(8,128)(2,1)S(1)}, bf16[256,576]{0,1:T(8,128)(2,1)}, u32[]{:S(2)}, u32[]{:S(2)}) collective-permute-start(bf16[256,576]{0,1:T(8,128)(2,1)S(1)} %all_gather.6), channel_id=1, source_target_pairs={{0,4},{4,8},{8,12},{12,16},{16,20},{20,24},{24,28},{1,5},{5,9},{9,... | collective-permute-start | bytes 884744 | tf_op jit(solution)/shard_map/ppermute | solution.py:16
  25.3 20.2 %all_gather.7 = bf16[256,1536]{1,0:T(8,128)(2,1)S(1)} all-gather(bf16[256,384]{1,0:T(8,128)(2,1)} %param.6), channel_id=1, replica_groups=mesh['ctx'=8,'head'=4] {'head'}, dimensions={1}, use_global_device_ids=true | all-gather | bytes 983040 | tf_op jit(solution)/shard_map/all_gather | solution.py:25
  45.5 3.3 %convolution_convert_fusion.3 = bf16[256,2048]{1,0:T(8,128)(2,1)} fusion(bf16[512,2048]{1,0:T(8,128)(2,1)} %param.10, bf16[256,576]{0,1:T(8,128)(2,1)S(1)} %all_gather.6), kind=kOutput, calls=%fused_computation.13 | convolution fusion | flops 537395200 | bytes 3407872 | tf_op jit(solution)/shard_map/dot_general | solution.py:37
  48.7 7.4 %convolution_convert_fusion = bf16[256,3072]{1,0:T(8,128)(2,1)} fusion(bf16[256,1536]{1,0:T(8,128)(2,1)S(1)} %all_gather.7, bf16[1536,3072]{1,0:T(8,128)(2,1)} %param.8), kind=kOutput, calls=%fused_computation.9 | convolution fusion | flops 2416705536 | bytes 11796480 | tf_op jit(solution)/shard_map/dot_general | solution.py:24
  56.1 0.7 fusion.15
  56.9 2.6 %copy.41 = bf16[256,3072]{0,1:T(8,128)(2,1)} copy(bf16[256,3072]{1,0:T(8,128)(2,1)} %convolution_convert_fusion) | data formatting | bytes 3145728 | tf_op jit(solution)/shard_map/convert_element_type | solution.py:29
  59.5 1.5 copy.46
  61.0 2.3 %copy.63 = bf16[256,2048]{0,1:T(8,128)(2,1)} copy(bf16[256,2048]{1,0:T(8,128)(2,1)} %convolution_convert_fusion.3) | data formatting | bytes 2097152 | tf_op jit(solution)/shard_map/reshape | solution.py:43
  63.3 1.7 fusion.7
  65.0 2.7 %convolution_convert_fusion.4 = bf16[256,2048]{1,0:T(8,128)(2,1)} fusion(bf16[512,2048]{1,0:T(8,128)(2,1)S(1)} %copy-done.2, bf16[256,576]{0,1:T(8,128)(2,1)} %collective-permute-done), kind=kOutput, calls=%fused_computation.14 | convolution fusion | flops 537395200 | bytes 3407872 | tf_op jit(solution)/shard_map/dot_general | solution.py:37
  67.6 2.3 %copy.62 = bf16[256,2048]{0,1:T(8,128)(2,1)} copy(bf16[256,2048]{1,0:T(8,128)(2,1)} %convolution_convert_fusion.4) | data formatting | bytes 2097152 | tf_op jit(solution)/shard_map/reshape | solution.py:43
  69.9 1.8 fusion.6
  71.7 0.3 bitcast_dynamic-update-slice_fusion.1
  72.0 0.3 bitcast_dynamic-update-slice_fusion
  72.3 0.8 copy-done.6
  73.1 4.5 %fusion.12 = f32[16,256,512]{2,1,0:T(8,128)} fusion(bf16[512,16,128]{2,0,1:T(8,128)(2,1)S(1)} %bitcast_dynamic-update-slice_fusion, bf16[256,16,192]{0,2,1:T(8,128)(2,1)S(1)} %bitcast.82), kind=kOutput, calls=%fused_computation.35 | convolution fusion | flops 536870912 | bytes 11534336 | tf_op jit(solution)/shard_map/qhd,khd->hqk/dot_general | solution.py:59
  77.6 0.8 slice.51
  78.4 10.6 %fusion.28 = (f32[16,256]{1,0:T(8,128)S(1)}, f32[16,256,512]{2,1,0:T(8,128)}) fusion(pred[256,512]{1,0:T(8,128)(4,1)S(1)} %copy-done.14, f32[16,256,512]{2,1,0:T(8,128)} %fusion.12, bf16[256,16,192]{0,2,1:T(8,128)(2,1)} %bitcast.81, bf16[256,64]{0,1:T(8,128)(2,1)S(1)} %slice.52, bf16[256,64]{0,1:T(8,128)(2,1)S(1)} %slice.51), kind=kOutput, calls=%fused_computation.58 | convolution fusion | flops 281149952 | bytes 17645568 | tf_op jit(solution)/shard_map/sub | solution.py:65
  89.0 3.9 %fusion.5 = bf16[16,256,512]{2,1,0:T(8,128)(2,1)S(1)} fusion(f32[16,256,512]{2,1,0:T(8,128)} %get-tuple-element.17, f32[16,256]{1,0:T(8,128)S(1)} %get-tuple-element.16), kind=kLoop, calls=%fused_computation.10 | loop fusion | flops 4194304 | bytes 12599296 | tf_op jit(solution)/shard_map/convert_element_type | solution.py:67
  92.9 0.7 convert_bitcast_fusion
  93.7 0.5 copy-done.11
  94.1 0.3 copy-done.12
  94.5 2.5 %multiply_reduce_fusion = (f32[256,16]{0,1:T(8,128)S(1)}, bf16[16,128,256]{2,1,0:T(8,128)(2,1)}) fusion(bf16[256,2048]{0,1:T(8,128)(2,1)S(1)} %copy.46, bf16[16,256,512]{2,1,0:T(8,128)(2,1)S(1)} %fusion.5, bf16[256,16,128]{0,2,1:T(8,128)(2,1)S(1)} %bitcast.93, bf16[256,16,128]{0,2,1:T(8,128)(2,1)S(1)} %bitcast.95), kind=kOutput, calls=%fused_computation.18 | convolution fusion | flops 543682560 | bytes 8404992 | tf_op jit(solution)/shard_map/hqk,khd->qhd/dot_general | solution.py:68
  96.9 0.2 slice-done.1
  97.2 2.3 %fusion.2 = bf16[16,256,512]{2,1,0:T(8,128)(2,1)S(1)} fusion(f32[16,256]{1,0:T(8,128)S(1)} %bitcast.101, f32[16,256,512]{2,1,0:T(8,128)S(1)} %bitcast.86, f32[16,256]{1,0:T(8,128)S(1)} %get-tuple-element.16, bf16[256,16,128]{0,2,1:T(8,128)(2,1)S(1)} %bitcast.88, bf16[256,16,128]{0,2,1:T(8,128)(2,1)S(1)} %bitcast.94, bf16[256,16,128]{0,2,1:T(8,128)(2,1)S(1)} %bitcast.96), kind=kOutput, calls=%fused_computation.3 | convolution fusion | flops 551550976 | bytes 15761408 | tf_op jit(solution)/shard_map/qhd,khd->hqk/dot_general | solution.py:72
  99.5 1.5 fusion.8
  101.1 1.0 copy-done.7
  102.1 0.8 fusion.9
  103.0 0.7 convert_bitcast_fusion.1
  103.8 1.6 fusion.26
  105.4 0.3 fusion.27
  105.7 1.6 fusion.33
  107.3 1.6 fusion.32
  108.9 0.1 copy.53
  109.1 2.9 %fusion.11 = bf16[256,512]{1,0:T(8,128)(2,1)S(1)} fusion(f32[256,512]{1,0:T(8,128)} %fusion.33, bf16[256,2048]{0,1:T(8,128)(2,1)} %bitcast.97, bf16[512,2048]{1,0:T(8,128)(2,1)} %param.10), kind=kOutput, calls=%fused_computation.31 | convolution fusion | flops 537133056 | bytes 3932160 | tf_op jit(solution)/shard_map/dot_general | solution.py:99
  112.0 1.3 collective-permute-start.1
  113.4 0.8 convolution_add_fusion.1
  114.1 1.4 collective-permute-done.1
  115.6 0.9 maximum_add_fusion
  116.5 2.1 %copy.64 = f32[256,576]{0,1:T(8,128)} copy(f32[256,576]{1,0:T(8,128)} %maximum_add_fusion) | data formatting | bytes 1179648
  118.7 3.6 %fusion.10 = bf16[256,16,64]{0,2,1:T(8,128)(2,1)S(1)} fusion(bf16[16,256,512]{2,1,0:T(8,128)(2,1)} %copy-done.1, bf16[256,64]{0,1:T(8,128)(2,1)S(1)} %slice.52, bf16[256,64]{0,1:T(8,128)(2,1)S(1)} %slice.51), kind=kOutput, calls=%fused_computation.28 | convolution fusion | flops 268828672 | bytes 4784128 | tf_op jit(solution)/shard_map/hqk,kr->qhr/dot_general | solution.py:76
  122.3 0.1 pad_maximum_fusion.1
  122.4 7.6 %fusion.31 = f32[256,1536]{1,0:T(8,128)} fusion(bf16[256,3072]{0,1:T(8,128)(2,1)S(1)} %bitcast.91, bf16[1536,3072]{1,0:T(8,128)(2,1)} %param.8), kind=kOutput, calls=%fused_computation.59 | convolution fusion | flops 2415919104 | bytes 12582912 | tf_op jit(solution)/shard_map/dot_general | solution.py:82
  130.0 1.2 copy-done.10
  131.2 1.4 copy.54
  132.6 13.0 %reduce-scatter.7.cloned.1.call-done = f32[144,256]{1,0:T(8,128)} async-done(((f32[576,256]{1,0:T(8,128)}), f32[144,256]{1,0:T(8,128)}) %reduce-scatter.7.cloned.1.call-update) | async-done | bytes 147472
  145.6 36.7 %reduce-scatter.5.cloned.1.call-done = f32[256,384]{1,0:T(8,128)} async-done(((f32[256,1536]{1,0:T(8,128)}), f32[256,384]{1,0:T(8,128)}) %reduce-scatter.5.cloned.1.call-update) | async-done | bytes 393232 | tf_op jit(solution)/shard_map/reduce_scatter | solution.py:113
  (41 shorter events, 0.5 us)
Async XLA Ops:
  7.2 56.1 %copy-start = (bf16[512,2048]{1,0:T(8,128)(2,1)S(1)}, bf16[512,2048]{1,0:T(8,128)(2,1)}, u32[]{:S(2)}) copy-start(bf16[512,2048]{1,0:T(8,128)(2,1)} %param.9) | copy-start | bytes 6291460
  7.2 138.4 %reduce-scatter.7.cloned.1.call-start = ((), (), s32[]{:S(2)}) async-start(), calls=%async_computation.3 | async-start | bytes 737280
  23.2 41.7 %collective-permute-start = (bf16[256,576]{0,1:T(8,128)(2,1)S(1)}, bf16[256,576]{0,1:T(8,128)(2,1)}, u32[]{:S(2)}, u32[]{:S(2)}) collective-permute-start(bf16[256,576]{0,1:T(8,128)(2,1)S(1)} %all_gather.6), channel_id=1, source_target_pairs={{0,4},{4,8},{8,12},{12,16},{16,20},{20,24},{24,28},{1,5},{5,9},{9,... | collective-permute-start | bytes 884744 | tf_op jit(solution)/shard_map/ppermute | solution.py:16
  63.3 1.7 copy-start.2
  69.9 2.1 %copy-start.8 = (bf16[32,16,8,128]{3,2,1,0:T(8,128)(2,1)S(1)}, bf16[32,16,8,128]{3,2,1,0:T(8,128)(2,1)}, u32[]{:S(2)}) copy-start(bf16[32,16,8,128]{3,2,1,0:T(8,128)(2,1)} %fusion.7) | copy-start | bytes 3145732
  71.7 1.4 copy-start.6
  72.3 5.3 %copy-start.4 = (bf16[512,16,128]{2,0,1:T(8,128)(2,1)}, bf16[512,16,128]{2,0,1:T(8,128)(2,1)S(1)}, u32[]{:S(2)}) copy-start(bf16[512,16,128]{2,0,1:T(8,128)(2,1)S(1)} %bitcast_dynamic-update-slice_fusion) | copy-start | bytes 6291460
  73.1 5.3 %copy-start.14 = (pred[256,512]{1,0:T(8,128)(4,1)S(1)}, pred[256,512]{1,0:T(8,128)(4,1)}, u32[]{:S(2)}) copy-start(pred[256,512]{1,0:T(8,128)(4,1)} %fusion.15) | copy-start | bytes 393220
  92.9 1.2 copy-start.11
  92.9 1.5 copy-start.12
  92.9 4.0 %slice-start = ((s8[8388608]{0:T(1024)(128)(4,1)}), s8[4194304]{0:T(1024)(128)(4,1)S(1)}, s32[]{:S(2)}) async-start(s8[8388608]{0:T(1024)(128)(4,1)} %bitcast.85), calls=%async_computation.4 | async-start | bytes 8388608
  94.5 2.7 %slice-start.1 = ((s8[8388608]{0:T(1024)(128)(4,1)}), s8[4194304]{0:T(1024)(128)(4,1)S(1)}, s32[]{:S(2)}) async-start(s8[8388608]{0:T(1024)(128)(4,1)} %bitcast.85), calls=%async_computation.5 | async-start | bytes 8388608
  97.2 2.3 %copy-start.5 = (bf16[512,16,128]{2,0,1:T(8,128)(2,1)S(1)}, bf16[512,16,128]{2,0,1:T(8,128)(2,1)}, u32[]{:S(2)}) copy-start(bf16[512,16,128]{2,0,1:T(8,128)(2,1)} %copy-done.4) | copy-start | bytes 6291460
  99.5 3.4 %copy-start.1 = (bf16[16,256,512]{2,1,0:T(8,128)(2,1)}, bf16[16,256,512]{2,1,0:T(8,128)(2,1)S(1)}, u32[]{:S(2)}) copy-start(bf16[16,256,512]{2,1,0:T(8,128)(2,1)S(1)} %fusion.2) | copy-start | bytes 12582916
  99.5 2.6 %copy-start.7 = (bf16[256,3072]{0,1:T(8,128)(2,1)S(1)}, bf16[256,3072]{0,1:T(8,128)(2,1)}, u32[]{:S(2)}) copy-start(bf16[256,3072]{0,1:T(8,128)(2,1)} %copy.41) | copy-start | bytes 4718596
  109.1 4.3 %copy-start.3 = (bf16[512,2048]{1,0:T(8,128)(2,1)S(1)}, bf16[512,2048]{1,0:T(8,128)(2,1)}, u32[]{:S(2)}) copy-start(bf16[512,2048]{1,0:T(8,128)(2,1)} %param.10) | copy-start | bytes 6291460
  109.1 4.3 %copy-start.9 = (bf16[256,16,128]{0,2,1:T(8,128)(2,1)S(1)}, bf16[256,16,128]{0,2,1:T(8,128)(2,1)}, u32[]{:S(2)}) copy-start(bf16[256,16,128]{0,2,1:T(8,128)(2,1)} %get-tuple-element.13) | copy-start | bytes 3145732
  109.1 4.3 %copy-start.13 = (f32[256,512]{1,0:T(8,128)S(1)}, f32[256,512]{1,0:T(8,128)}, u32[]{:S(2)}) copy-start(f32[256,512]{1,0:T(8,128)} %fusion.32) | copy-start | bytes 1572868
  112.0 3.5 %collective-permute-start.1 = (bf16[256,576]{1,0:T(8,128)(2,1)S(1)}, bf16[256,576]{1,0:T(8,128)(2,1)S(1)}, u32[]{:S(2)}, u32[]{:S(2)}) collective-permute-start(bf16[256,576]{1,0:T(8,128)(2,1)S(1)} %pad_maximum_fusion.4), channel_id=1, source_target_pairs={{4,0},{8,4},{12,8},{16,12},{20,16},{24,20},{28,24},{5,1},{9,5},{13... | collective-permute-start | bytes 884744 | tf_op jit(solution)/shard_map/ppermute | solution.py:16
  118.6 63.6 %reduce-scatter.5.cloned.1.call-start = ((), (), s32[]{:S(2)}) async-start(), calls=%async_computation.2 | async-start | bytes 1966080 | tf_op jit(solution)/shard_map/reduce_scatter | solution.py:113
  129.9 1.2 copy-start.10
Sparse Core Ops, SparseCore 0:
  118.8 26.7 reduce-scatter.6
  148.4 33.7 reduce-scatter.4
where the time goes:
time: 190 us; the launch traced here: 189 us
  matrix products  58.5 us (31%)
  waiting for transfers between devices  51.1 us (27%)
  blocking collectives  36.2 us (19%)
  local copies, waits for them, and re-layouts  19.7 us (10%)
  between operations  14.3 us (8%)
  other arithmetic  5.84 us (3%)
  starting transfers between devices  3.38 us (2%)
    reduce_scatter x1, waiting for transfers between devices, on_device(): lax.psum_scatter(grad_qpart, 'head', scatter_dimension=1, tiled=True)  36.7 us
    all_gather x1, blocking collectives, on_device(): lax.all_gather(q_latent, 'head', axis=1, tiled=True)  20.2 us
    all_gather x1, blocking collectives, on_device(): latent = lax.all_gather(kv_latent, 'head', axis=1, tiled=True)  16 us
    unnamed x3, waiting for transfers between devices  13 us
    sub x1, matrix products, on_device(): expons = jnp.where(visible, jnp.exp(scores - maxima), jnp.float32(0.0))  10.6 us
    unnamed x38, local copies, waits for them, and re-layouts  9.38 us
    dot_general x1, matrix products, on_device(): jnp.dot(grad_query, w_query.T, preferred_element_type=jnp.float32)  7.55 us
    dot_general x1, matrix products, on_device(): jnp.dot(lax.all_gather(q_latent, 'head', axis=1, tiled=True), w_query, pr...  7.4 us
  transfers between devices with their start and end apart: 4, of which 3 were waited for; matrix products, arithmetic and copies ran while one was open for 17% of the time, Pallas kernels for 0%

commit v1 on v0

v1 whole, which is shorter than its diff:
```python
import functools
import math

import jax
import jax.numpy as jnp
from jax import lax
from jax.experimental import pallas as pl
from jax.experimental.pallas import tpu as pltpu
from jax.sharding import PartitionSpec as P

KVL = 512
ROPE = 64
NOPE = 128
VDIM = 128
WIDTH = NOPE + ROPE
SCALE = WIDTH ** (-0.5)
F32 = jnp.float32
BF16 = jnp.bfloat16
MESH = pl.DeviceIdType.MESH


def nn(a, b):
    return jnp.dot(a, b, preferred_element_type=F32)


def nt(a, b):
    return lax.dot_general(a, b, (((1,), (1,)), ((), ())), preferred_element_type=F32)


def kernel(
    n_ctx, n_head,
    q_ref, kv_ref, do_ref, wq_hbm, wk_hbm, wv_hbm,
    out_ref, gq_ref, gkv_ref,
    wq, wk, wv, wkt, wvt, dot_t, q_in, kv_in, kv_prev, lat, lat_t, q_acc, q_t,
    keys, keys_t, values, values_t, gq_t, gk, gv, krope, back_out, back_in,
    rq_out, rq_in, rkv_out, rkv_in, gkv_own, gq_own,
    w_sem, kv_send, kv_recv, q_send, q_recv, p_send, p_recv,
    b_send, b_recv, rq_send, rq_recv, rkv_send, rkv_recv,
):
    ctx = lax.axis_index("ctx")
    me = lax.axis_index("head")
    rows, q_cols = q_ref.shape
    kv_cols = kv_ref.shape[1]
    heads = wk.shape[1] // NOPE
    after = lax.rem(ctx + 1, n_ctx)
    before = lax.rem(ctx + n_ctx - 1, n_ctx)
    order = sorted(range(1, n_head), key=lambda s: (min(s, n_head - s), s))

    loads = [
        pltpu.make_async_copy(src, dst, w_sem.at[i])
        for i, (src, dst) in enumerate(((wk_hbm, wk), (wv_hbm, wv), (wq_hbm, wq)))
    ]
    for load in loads:
        load.start()

    barrier = pltpu.get_barrier_semaphore()
    for s in range(1, n_head):
        pl.semaphore_signal(barrier, inc=1, device_id={"head": lax.rem(me + s, n_head)}, device_id_type=MESH)
    pl.semaphore_signal(barrier, inc=1, device_id={"ctx": after}, device_id_type=MESH)
    pl.semaphore_signal(barrier, inc=1, device_id={"ctx": before}, device_id_type=MESH)
    pl.semaphore_wait(barrier, n_head + 1)

    def send(src, dst, send_sem, recv_sem, device):
        copy = pltpu.make_async_remote_copy(
            src_ref=src, dst_ref=dst, send_sem=send_sem, recv_sem=recv_sem,
            device_id=device, device_id_type=MESH,
        )
        copy.start()
        return copy

    def peer(s):
        return {"head": lax.rem(me + s, n_head)}

    kv_copies = {s: send(kv_ref, kv_in.at[s], kv_send.at[s], kv_recv.at[s], peer(s)) for s in order}
    p_copies = {0: send(kv_ref, kv_prev.at[0], p_send.at[0], p_recv.at[0], {"ctx": after})}
    q_copies = {s: send(q_ref, q_in.at[s], q_send.at[s], q_recv.at[s], peer(s)) for s in order}

    @pl.loop(0, heads)
    def _(h):
        at = pl.multiple_of(h * VDIM, VDIM)
        dot_t[pl.ds(at, VDIM), :] = do_ref[:, pl.ds(at, VDIM)].T

    loads[0].wait()

    @pl.loop(0, heads)
    def _(h):
        at = pl.multiple_of(h * NOPE, NOPE)
        wkt[pl.ds(at, NOPE), :] = wk[:, pl.ds(at, NOPE)].T

    loads[1].wait()

    @pl.loop(0, heads)
    def _(h):
        at = pl.multiple_of(h * VDIM, VDIM)
        wvt[pl.ds(at, VDIM), :] = wv[:, pl.ds(at, VDIM)].T

    loads[2].wait()

    def add_queries(block, s, first):
        owner = lax.rem(me + n_head - s, n_head)
        at = pl.multiple_of(owner * q_cols, q_cols)
        tile = 2 * WIDTH

        @pl.loop(0, wq.shape[1] // tile)
        def _(j):
            cols = pl.ds(pl.multiple_of(j * tile, tile), tile)
            part = nn(block[...], wq[pl.ds(at, q_cols), cols])
            if first:
                q_acc[:, cols] = part
            else:
                q_acc[:, cols] += part

    add_queries(q_ref, 0, True)

    for s in order:
        kv_copies[s].wait_recv()
        p_copies[s] = send(kv_in.at[s], kv_prev.at[s], p_send.at[s], p_recv.at[s], {"ctx": after})

    def assemble(parts, row):
        width = n_head * kv_cols
        total = None
        total_t = None
        for s in range(n_head):
            owner = lax.rem(me + n_head - s, n_head)
            src = lax.broadcasted_iota(jnp.int32, (kv_cols, width), 0) + owner * kv_cols
            dst = lax.broadcasted_iota(jnp.int32, (kv_cols, width), 1)
            place = jnp.where(src == dst, F32(1.0), F32(0.0)).astype(BF16)
            src_t = lax.broadcasted_iota(jnp.int32, (ROPE, kv_cols), 1) + owner * kv_cols
            dst_t = lax.broadcasted_iota(jnp.int32, (ROPE, kv_cols), 0) + KVL
            place_t = jnp.where(src_t == dst_t, F32(1.0), F32(0.0)).astype(BF16)
            term = nn(parts[s], place)
            term_t = nt(place_t, parts[s])
            total = term if total is None else total + term
            total_t = term_t if total_t is None else total_t + term_t
        lat[row:row + rows, :] = total.astype(BF16)
        lat_t[:, row:row + rows] = total_t.astype(BF16)

    def expand(row):
        tile = 2 * NOPE

        @pl.loop(0, heads // 2)
        def _(j):
            cols = pl.ds(pl.multiple_of(j * tile, tile), tile)
            main = lat[row:row + rows, :KVL]
            keys[row:row + rows, cols] = nn(main, wk[:, cols]).astype(BF16)
            values[row:row + rows, cols] = nn(main, wv[:, cols]).astype(BF16)
            keys_t[cols, row:row + rows] = nt(wkt[cols, :], main).astype(BF16)
            values_t[cols, row:row + rows] = nt(wvt[cols, :], main).astype(BF16)

    assemble([kv_ref[...]] + [kv_in[s] for s in range(1, n_head)], rows)
    expand(rows)
    for s in range(n_head):
        p_copies[s].wait_recv()
    assemble([kv_prev[s] for s in range(n_head)], 0)
    expand(0)

    for s in order:
        q_copies[s].wait_recv()
        add_queries(q_in.at[s], s, False)

    @pl.loop(0, wq.shape[1] // NOPE)
    def _(j):
        at = pl.multiple_of(j * NOPE, NOPE)
        q_t[pl.ds(at, NOPE), :] = q_acc[:, pl.ds(at, NOPE)].astype(BF16).T

    krope[...] = jnp.zeros_like(krope)

    @pl.loop(0, heads)
    def _(h):
        at = pl.multiple_of(h * NOPE, NOPE)
        q_at = pl.ds(pl.multiple_of(h * WIDTH, WIDTH), WIDTH)
        cols = pl.ds(at, NOPE)
        query_t = q_t[q_at, :]
        key = jnp.concatenate([keys[:, cols], lat[:, KVL:]], 1)
        scores = nn(key, query_t)
        key_pos = lax.broadcasted_iota(jnp.int32, (2 * rows, rows), 0)
        query_pos = lax.broadcasted_iota(jnp.int32, (2 * rows, rows), 1)
        low = jnp.where(ctx == 0, rows, 0)
        visible = (key_pos >= low) & (key_pos - rows <= query_pos)
        scores = jnp.where(visible, scores, F32(-1e30))
        top = jnp.max(scores, 0, keepdims=True)
        expons = jnp.exp2((scores - top) * F32(SCALE * math.log2(math.e)))
        probs = expons * (F32(1.0) / jnp.sum(expons, 0, keepdims=True))
        probs_b = probs.astype(BF16)
        result = nn(values_t[cols, :], probs_b).astype(BF16)
        out_ref[cols, :] = result
        grad_out = dot_t[cols, :]
        row_dot = jnp.sum(grad_out.astype(F32) * result.astype(F32), 0, keepdims=True)
        dprob = nn(values[:, cols], grad_out)
        dscore = (probs * (dprob - row_dot) * F32(SCALE)).astype(BF16)
        key_t = jnp.concatenate([keys_t[cols, :], lat_t[...]], 0)
        gq_t[q_at, :] = nn(key_t, dscore).astype(BF16)
        gk[:, cols] = nt(dscore, query_t[:NOPE]).astype(BF16)
        krope[:, :rows] += nt(query_t[NOPE:], dscore[:rows]).astype(BF16).astype(F32)
        krope[:, rows:] += nt(query_t[NOPE:], dscore[rows:]).astype(BF16).astype(F32)
        gv[:, cols] = nt(probs_b, grad_out).astype(BF16)

    def project(row):
        return nt(wk[...], gk[row:row + rows, :]) + nt(wv[...], gv[row:row + rows, :])

    back_out[:KVL, :] = project(0).astype(BF16)
    back_out[KVL:, :] = krope[:, :rows].astype(BF16)
    back = send(back_out, back_in, b_send, b_recv, {"ctx": before})

    def query_part(s):
        at = pl.multiple_of(lax.rem(me + s, n_head) * q_cols, q_cols)
        return nn(wq[pl.ds(at, q_cols), :], gq_t[...])

    rq_copies = {}
    for s in order[::-1]:
        rq_out[s] = query_part(s).astype(BF16)
        rq_copies[s] = send(rq_out.at[s], rq_in.at[s], rq_send.at[s], rq_recv.at[s], peer(s))

    gkv_own[:KVL, :] = project(rows)
    gkv_own[KVL:, :] = krope[:, rows:]
    back.wait_recv()
    gkv_own[...] += back_in[...].astype(F32)

    def kv_part(s):
        at = pl.multiple_of(lax.rem(me + s, n_head) * kv_cols, kv_cols)
        return gkv_own[pl.ds(at, kv_cols), :]

    rkv_copies = {}
    for s in order[::-1]:
        rkv_out[s] = kv_part(s).astype(BF16)
        rkv_copies[s] = send(rkv_out.at[s], rkv_in.at[s], rkv_send.at[s], rkv_recv.at[s], peer(s))

    gq_own[...] = query_part(0)
    for s in order:
        rq_copies[s].wait_recv()
        gq_own[...] += rq_in[s].astype(F32)
    gq_ref[...] = gq_own[...]
    total = kv_part(0)
    for s in order:
        rkv_copies[s].wait_recv()
        total = total + rkv_in[s].astype(F32)
    gkv_ref[...] = total

    for s in order:
        kv_copies[s].wait_send()
        q_copies[s].wait_send()
        rq_copies[s].wait_send()
        rkv_copies[s].wait_send()
    for s in range(n_head):
        p_copies[s].wait_send()
    back.wait_send()


def on_device(n_ctx, n_head, q_latent, kv_latent, w_query, w_key, w_value, d_out):
    rows, q_cols = q_latent.shape
    kv_cols = kv_latent.shape[1]
    ql, qw = w_query.shape
    kw = w_key.shape[1]
    kvw = n_head * kv_cols
    vmem = pl.BlockSpec(memory_space=pltpu.VMEM)
    hbm = pl.BlockSpec(memory_space=pl.ANY)
    dma = pltpu.SemaphoreType.DMA
    out_t, gq_t, gkv_t = pl.pallas_call(
        functools.partial(kernel, n_ctx, n_head),
        out_shape=(
            jax.ShapeDtypeStruct((kw, rows), BF16),
            jax.ShapeDtypeStruct((q_cols, rows), F32),
            jax.ShapeDtypeStruct((kv_cols, rows), F32),
        ),
        in_specs=[vmem, vmem, vmem, hbm, hbm, hbm],
        out_specs=(vmem, vmem, vmem),
        scratch_shapes=[
            pltpu.VMEM((ql, qw), BF16),
            pltpu.VMEM((KVL, kw), BF16),
            pltpu.VMEM((KVL, kw), BF16),
            pltpu.VMEM((kw, KVL), BF16),
            pltpu.VMEM((kw, KVL), BF16),
            pltpu.VMEM((kw, rows), BF16),
            pltpu.VMEM((n_head, rows, q_cols), BF16),
            pltpu.VMEM((n_head, rows, kv_cols), BF16),
            pltpu.VMEM((n_head, rows, kv_cols), BF16),
            pltpu.VMEM((2 * rows, kvw), BF16),
            pltpu.VMEM((ROPE, 2 * rows), BF16),
            pltpu.VMEM((rows, qw), F32),
            pltpu.VMEM((qw, rows), BF16),
            pltpu.VMEM((2 * rows, kw), BF16),
            pltpu.VMEM((kw, 2 * rows), BF16),
            pltpu.VMEM((2 * rows, kw), BF16),
            pltpu.VMEM((kw, 2 * rows), BF16),
            pltpu.VMEM((qw, rows), BF16),
            pltpu.VMEM((2 * rows, kw), BF16),
            pltpu.VMEM((2 * rows, kw), BF16),
            pltpu.VMEM((ROPE, 2 * rows), F32),
            pltpu.VMEM((kvw, rows), BF16),
            pltpu.VMEM((kvw, rows), BF16),
            pltpu.VMEM((n_head, q_cols, rows), BF16),
            pltpu.VMEM((n_head, q_cols, rows), BF16),
            pltpu.VMEM((n_head, kv_cols, rows), BF16),
            pltpu.VMEM((n_head, kv_cols, rows), BF16),
            pltpu.VMEM((kvw, rows), F32),
            pltpu.VMEM((q_cols, rows), F32),
            dma((3,)),
            dma((n_head,)), dma((n_head,)),
            dma((n_head,)), dma((n_head,)),
            dma((n_head,)), dma((n_head,)),
            dma, dma,
            dma((n_head,)), dma((n_head,)),
            dma((n_head,)), dma((n_head,)),
        ],
        compiler_params=pltpu.CompilerParams(
            collective_id=0, has_side_effects=True, vmem_limit_bytes=60 * 1024 * 1024,
        ),
        name="latent_attention",
    )(q_latent, kv_latent, d_out, w_query, w_key, w_value)
    return out_t.T, gq_t.T, gkv_t.T


def solution(mesh):
    return jax.shard_map(
        functools.partial(on_device, mesh.shape["ctx"], mesh.shape["head"]),
        mesh=mesh,
        in_specs=(
            P("ctx", "head"),
            P("ctx", "head"),
            P(None, "head"),
            P(None, "head"),
            P(None, "head"),
            P("ctx", "head"),
        ),
        out_specs=(P("ctx", "head"), P("ctx", "head"), P("ctx", "head")),
        check_vma=False,
    )
```

time: 190 us -> 92.6 us (0.49)
  Pallas kernels: 0 us -> 86.2 us
  matrix products: 58.5 us -> 0 us
  waiting for transfers between devices: 51.1 us -> 0 us
  blocking collectives: 36.2 us -> 0 us
  local copies, waits for them, and re-layouts: 19.7 us -> 5.55 us
  between operations: 14.3 us -> 0.66 us
  other arithmetic: 5.84 us -> 0 us
  starting transfers between devices: 3.38 us -> 0 us
    pallas_call x0 -> x1, Pallas kernels: none -> 86.2 us  [on_device(): pl.pallas_call(functools.partial(kernel, n_ctx, n_head), out_shape=(jax.S...]
    dot_general x18 -> x0, matrix products: 47.9 us -> none  [the longest x1 7.55 us: on_device(): jnp.dot(grad_query, w_query.T, preferred_element_type=jnp.float32)]
    reduce_scatter x1 -> x0, waiting for transfers between devices: 36.7 us -> none  [on_device(): lax.psum_scatter(grad_qpart, 'head', scatter_dimension=1, tiled=True)]
    all_gather x2 -> x0, blocking collectives: 36.2 us -> none  [the longest x1 20.2 us: on_device(): lax.all_gather(q_latent, 'head', axis=1, tiled=True)]
    unnamed x3 -> x0, waiting for transfers between devices: 13 us -> none
    sub x1 -> x0, matrix products: 10.6 us -> none  [on_device(): expons = jnp.where(visible, jnp.exp(scores - maxima), jnp.float32(0.0))]
    reshape x2 -> x0, local copies, waits for them, and re-layouts: 4.57 us -> none  [expand(): values.reshape(block_rows, per_dev, VDIM)]
    convert_element_type x1 -> x0, other arithmetic: 3.85 us -> none  [on_device(): probs_b = probs.astype(jnp.bfloat16)]
  transfers between devices with their start and end apart: 4 -> 0, of which waited for: 3 -> 0; matrix products, arithmetic and copies ran while one was open for 17% -> 0% of each run, Pallas kernels for 0% -> 0%
where the time goes in v1:
time: 92.6 us; the launch traced here: 92.4 us
  Pallas kernels  86.2 us (93%)
  local copies, waits for them, and re-layouts  5.55 us (6%)
    pallas_call x1, Pallas kernels, on_device(): pl.pallas_call(functools.partial(kernel, n_ctx, n_head), out_shape=(jax.S...  86.2 us
    unnamed x8, local copies, waits for them, and re-layouts  5.55 us

profile of v1, /device:TPU:0, one launch (start us, length us, event | category | flops | bytes accessed | tf_op | source)
XLA Modules:
  0.0 92.4 jit_solution(5636516443265834915)
XLA Ops:
  0.6 1.6 %copy.9.kv_ref = bf16[256,144]{1,0:T(8,128)(2,1)} copy(bf16[256,144]{0,1:T(8,128)(2,1)} %param.7) | data formatting | bytes 147456 | tf_op args[1]
  2.3 86.2 %latent_attention.1 = (bf16[2048,256]{1,0:T(8,128)(2,1)}, f32[384,256]{1,0:T(8,128)}, f32[144,256]{1,0:T(8,128)}) custom-call(bf16[256,384]{1,0:T(8,128)(2,1)} %q_ref.1, bf16[256,144]{1,0:T(8,128)(2,1)} %copy.9.kv_ref, bf16[256,2048]{1,0:T(8,128)(2,1)} %do_ref.1, bf16[1536,3072]{1,0:T(8,128)(2,1)} %wq_hbm.1, bf16[512,2048]{1,0:T(8,128)(2,1)} %wk_hbm.1, ...), custom_call_target="tpu_custom_call" | custom-call | tf_op jit(solution)/shard_map/latent_attention/pallas_call | solution.py:258
  88.5 0.0 copy-start
  88.5 0.0 copy-start.1
  88.5 2.3 %copy.10 = bf16[256,2048]{1,0:T(8,128)(2,1)} copy(bf16[256,2048]{0,1:T(8,128)(2,1)} %bitcast.3) | data formatting | bytes 2097152
  90.8 0.0 copy-done
  90.8 0.9 copy.11
  91.8 0.0 copy-done.1
  91.8 0.7 copy.13
Async XLA Ops:
  88.5 2.3 %copy-start = (f32[384,256]{1,0:T(8,128)S(1)}, f32[384,256]{1,0:T(8,128)}, u32[]{:S(2)}) copy-start(f32[384,256]{1,0:T(8,128)} %get-tuple-element.7) | copy-start | bytes 1179652
  88.5 3.3 %copy-start.1 = (f32[144,256]{1,0:T(8,128)S(1)}, f32[144,256]{1,0:T(8,128)}, u32[]{:S(2)}) copy-start(f32[144,256]{1,0:T(8,128)} %get-tuple-element.8) | copy-start | bytes 442372

commit v2 on v1

v2 whole, which is shorter than its diff:
```python
import functools
import math

import jax
import jax.numpy as jnp
from jax import lax
from jax.experimental import pallas as pl
from jax.experimental.pallas import tpu as pltpu
from jax.sharding import PartitionSpec as P

KVL = 512
ROPE = 64
NOPE = 128
VDIM = 128
WIDTH = NOPE + ROPE
SCALE = WIDTH ** (-0.5)
F32 = jnp.float32
BF16 = jnp.bfloat16
MESH = pl.DeviceIdType.MESH


def nn(a, b):
    return jnp.dot(a, b, preferred_element_type=F32)


def nt(a, b):
    return lax.dot_general(a, b, (((1,), (1,)), ((), ())), preferred_element_type=F32)


def kernel(
    n_ctx, n_head, chunks,
    q_ref, kv_ref, do_ref, wq_hbm, wk_hbm, wv_hbm,
    out_ref, gq_ref, gkv_ref,
    wq, wk, wv, wkt, wvt, dot_t, q_in, kv_in, kv_prev, lat, lat_t, q_acc, q_t,
    keys, keys_t, values, values_t, gq_t, gk, gv, gk_sum, gv_sum, kr_sum, krope, back_out, back_in,
    rq_out, rq_right, rq_left, rkv_out, rkv_right, rkv_left, gkv_own, stage_right, stage_left,
    bias, w_sem, kv_r, kv_l, kv_recv, q_r, q_l, q_recv, p_send, p_recv,
    b_send, b_recv, rq_send, rq_rr, rq_rl, rkv_send, rkv_rr, rkv_rl,
):
    ctx = lax.axis_index("ctx")
    me = lax.axis_index("head")
    last = n_head - 1
    rows, q_cols = q_ref.shape
    part_rows = rows // chunks
    kv_cols = kv_ref.shape[0]
    heads = wk.shape[1] // NOPE
    after = {"ctx": lax.rem(ctx + 1, n_ctx)}
    before = {"ctx": lax.rem(ctx + n_ctx - 1, n_ctx)}
    right = {"head": jnp.minimum(me + 1, last)}
    left = {"head": jnp.maximum(me - 1, 0)}
    has_right = me < last
    has_left = me > 0

    loads = [
        pltpu.make_async_copy(src, dst, w_sem.at[i])
        for i, (src, dst) in enumerate(((wk_hbm, wk), (wv_hbm, wv), (wq_hbm, wq)))
    ]
    for load in loads:
        load.start()

    barrier = pltpu.get_barrier_semaphore()

    @pl.when(has_right)
    def _():
        pl.semaphore_signal(barrier, inc=1, device_id=right, device_id_type=MESH)

    @pl.when(has_left)
    def _():
        pl.semaphore_signal(barrier, inc=1, device_id=left, device_id_type=MESH)

    pl.semaphore_signal(barrier, inc=1, device_id=after, device_id_type=MESH)
    pl.semaphore_signal(barrier, inc=1, device_id=before, device_id_type=MESH)
    pl.semaphore_wait(barrier, 2 + jnp.minimum(me, 1) + jnp.minimum(last - me, 1))

    def copy_of(src, dst, send_sem, recv_sem, device):
        return pltpu.make_async_remote_copy(
            src_ref=src, dst_ref=dst, send_sem=send_sem, recv_sem=recv_sem,
            device_id=device, device_id_type=MESH,
        )

    class Gather:
        def __init__(self, own, slots, send_r, send_l, recv):
            self.own, self.slots, self.recv = own, slots, recv
            self.send_r, self.send_l = send_r, send_l

        def moves(self, t, act):
            @pl.when(has_right & (me >= t))
            def _():
                owner = me - t
                src = self.own if t == 0 else self.slots(owner)
                act(copy_of(src, self.slots(owner), self.send_r(t), self.recv(owner), right))

            @pl.when(has_left & (me + t <= last))
            def _():
                owner = me + t
                src = self.own if t == 0 else self.slots(owner)
                act(copy_of(src, self.slots(owner), self.send_l(t), self.recv(owner), left))

        def start(self, t):
            if t < last:
                self.moves(t, lambda copy: copy.start())

        def each(self, t, act):
            @pl.when(me - 1 - t >= 0)
            def _():
                act(me - 1 - t)

            @pl.when(me + 1 + t <= last)
            def _():
                act(me + 1 + t)

        def arrive(self, t, act=None):
            def wait(owner):
                slot = self.slots(owner)
                copy_of(slot, slot, self.send_r(0), self.recv(owner), right).wait_recv()
                if act is not None:
                    act(owner)

            self.each(t, wait)
            self.start(t + 1)

        def finish(self):
            for t in range(last):
                self.moves(t, lambda copy: copy.wait_send())

    def pass_on(owner, src):
        copy_of(src, kv_prev.at[owner], p_send.at[owner], p_recv.at[owner], after).start()

    kv_gather = Gather(kv_ref, lambda i: kv_in.at[i], lambda t: kv_r.at[t], lambda t: kv_l.at[t], lambda i: kv_recv.at[i])
    q_gathers = [
        Gather(
            q_ref.at[pl.ds(c * part_rows, part_rows), :],
            lambda i, c=c: q_in.at[c, i],
            lambda t, c=c: q_r.at[c, t],
            lambda t, c=c: q_l.at[c, t],
            lambda i, c=c: q_recv.at[c, i],
        )
        for c in range(chunks)
    ]
    kv_gather.start(0)
    pass_on(me, kv_ref)
    for gather in q_gathers:
        gather.start(0)
    kv_in[me] = kv_ref[...]

    key_pos = lax.broadcasted_iota(jnp.int32, (2 * rows, rows), 0)
    query_pos = lax.broadcasted_iota(jnp.int32, (2 * rows, rows), 1)
    low = jnp.where(ctx == 0, rows, 0)
    visible = (key_pos >= low) & (key_pos - rows <= query_pos)
    bias[...] = jnp.where(visible, F32(0.0), F32(-1e30))
    loads[0].wait()

    @pl.loop(0, heads)
    def _(h):
        at = pl.multiple_of(h * NOPE, NOPE)
        wkt[pl.ds(at, NOPE), :] = wk[:, pl.ds(at, NOPE)].T

    def kv_step(t):
        kv_gather.arrive(t, lambda owner: pass_on(owner, kv_in.at[owner]))

    def q_step(c, t):
        q_gathers[c].arrive(t)

    kv_step(0)
    loads[1].wait()

    @pl.loop(0, heads)
    def _(h):
        at = pl.multiple_of(h * VDIM, VDIM)
        wvt[pl.ds(at, VDIM), :] = wv[:, pl.ds(at, VDIM)].T

    def add_queries(c, block, owner, first=False):
        at = pl.multiple_of(owner * q_cols, q_cols)
        span = pl.ds(c * part_rows, part_rows)
        tile = 2 * WIDTH

        @pl.loop(0, wq.shape[1] // tile)
        def _(j):
            cols = pl.ds(pl.multiple_of(j * tile, tile), tile)
            part = nn(block[...], wq[pl.ds(at, q_cols), cols])
            if first:
                q_acc[span, cols] = part
            else:
                q_acc[span, cols] += part

    def add_arrived(c, t):
        q_gathers[c].each(t, lambda owner: add_queries(c, q_in.at[c, owner], owner))

    def assemble(parts, row):
        width = n_head * kv_cols
        total = None
        for i in range(n_head):
            dst = lax.broadcasted_iota(jnp.int32, (width, kv_cols), 0)
            src = lax.broadcasted_iota(jnp.int32, (width, kv_cols), 1) + i * kv_cols
            place = jnp.where(src == dst, F32(1.0), F32(0.0)).astype(BF16)
            term = nn(place, parts[i])
            total = term if total is None else total + term
        total = total.astype(BF16)
        span = slice(row, row + rows)
        lat_t[:, span] = total
        lat[span, :KVL] = total[:KVL].T
        lat[span, KVL:] = total[KVL:].T

    def expand(row):
        tile = 2 * NOPE
        span = slice(row, row + rows)

        @pl.loop(0, heads // 2)
        def _(j):
            cols = pl.ds(pl.multiple_of(j * tile, tile), tile)
            main = lat[span, :KVL]
            main_t = lat_t[:KVL, span]
            keys[span, cols] = nn(main, wk[:, cols]).astype(BF16)
            values[span, cols] = nn(main, wv[:, cols]).astype(BF16)
            keys_t[cols, span] = nn(wkt[cols, :], main_t).astype(BF16)
            values_t[cols, span] = nn(wvt[cols, :], main_t).astype(BF16)

    def finish_queries(c):
        @pl.loop(0, wq.shape[1] // NOPE)
        def _(j):
            at = pl.multiple_of(j * NOPE, NOPE)
            span = slice(c * part_rows, (c + 1) * part_rows)
            q_t[pl.ds(at, NOPE), span] = q_acc[span, pl.ds(at, NOPE)].astype(BF16).T

    if last > 0:
        q_step(0, 0)

    @pl.loop(0, heads)
    def _(h):
        at = pl.multiple_of(h * VDIM, VDIM)
        dot_t[pl.ds(at, VDIM), :] = do_ref[:, pl.ds(at, VDIM)].T

    loads[2].wait()
    for c in range(chunks):
        add_queries(c, q_ref.at[pl.ds(c * part_rows, part_rows), :], me, True)
    for t in range(1, last):
        kv_step(t)
        add_arrived(0, t - 1)
        if t < last - 1:
            q_step(0, t)
    assemble([kv_in[i] for i in range(n_head)], rows)
    expand(rows)
    for i in range(n_head):
        copy_of(kv_ref, kv_prev.at[i], p_send.at[i], p_recv.at[i], after).wait_recv()
    assemble([kv_prev[i] for i in range(n_head)], 0)
    expand(0)
    if last > 1:
        q_step(0, last - 1)
    if last > 0:
        add_arrived(0, last - 1)
    finish_queries(0)
    krope[...] = jnp.zeros_like(krope)

    def attend(c, h):
        seen = rows + (c + 1) * part_rows
        span = slice(c * part_rows, (c + 1) * part_rows)
        at = pl.multiple_of(h * NOPE, NOPE)
        q_at = pl.ds(pl.multiple_of(h * WIDTH, WIDTH), WIDTH)
        cols = pl.ds(at, NOPE)
        query_t = q_t[q_at, span]
        key = jnp.concatenate([keys[:seen, cols], lat[:seen, KVL:]], 1)
        scores = nn(key, query_t)
        scores = scores + bias[:seen, span]
        top = jnp.max(scores, 0, keepdims=True)
        expons = jnp.exp2((scores - top) * F32(SCALE * math.log2(math.e)))
        probs = expons * (F32(1.0) / jnp.sum(expons, 0, keepdims=True))
        probs_b = probs.astype(BF16)
        result = nn(values_t[cols, :seen], probs_b).astype(BF16)
        out_ref[cols, span] = result
        grad_out = dot_t[cols, span]
        row_dot = jnp.sum(grad_out.astype(F32) * result.astype(F32), 0, keepdims=True)
        dprob = nn(values[:seen, cols], grad_out)
        dscore = (probs * (dprob - row_dot) * F32(SCALE)).astype(BF16)
        key_t = jnp.concatenate([keys_t[cols, :seen], lat_t[KVL:, :seen]], 0)
        gq_t[q_at, span] = nn(key_t, dscore).astype(BF16)
        g_key = nt(dscore, query_t[:NOPE])
        g_rope = nt(query_t[NOPE:], dscore)
        g_value = nt(probs_b, grad_out)
        if c > 0:
            before_rows = rows + c * part_rows
            g_key = jnp.concatenate([g_key[:before_rows] + gk_sum[:, cols], g_key[before_rows:]], 0)
            g_value = jnp.concatenate([g_value[:before_rows] + gv_sum[:, cols], g_value[before_rows:]], 0)
            g_rope = jnp.concatenate([g_rope[:, :before_rows] + kr_sum[h], g_rope[:, before_rows:]], 1)
        if c + 1 < chunks:
            gk_sum[:, cols] = g_key
            gv_sum[:, cols] = g_value
            kr_sum[h] = g_rope
        else:
            gk[:, cols] = g_key.astype(BF16)
            gv[:, cols] = g_value.astype(BF16)
            krope[...] += g_rope.astype(BF16).astype(F32)

    def attention(c, hooks):
        groups = max(1, len(hooks) + 1)
        edges = [heads * g // groups for g in range(groups + 1)]
        for g in range(groups):
            @pl.loop(edges[g] // UNROLL, edges[g + 1] // UNROLL)
            def _(h):
                for u in range(UNROLL):
                    attend(c, h * UNROLL + u)

            if g < len(hooks):
                hooks[g]()

    class Reduce:
        def __init__(self, part, out, in_right, in_left, send, recv_right, recv_left, stages):
            self.part, self.out, self.send = part, out, send
            self.ways = (
                (in_right, recv_right, right, stages[0], has_left),
                (in_left, recv_left, left, stages[1], has_right),
            )

        def step(self, tick):
            for way, (slots, recv, device, stage, joined) in enumerate(self.ways):
                lag = me if way == 0 else last - me
                owner = last - (tick - lag) if way == 0 else tick - lag

                @pl.when(tick >= lag)
                def _():
                    stage[...] = self.part(owner)

                    @pl.when(joined)
                    def _():
                        copy_of(slots(owner), slots(owner), self.send(owner), recv(owner), device).wait_recv()
                        stage[...] += slots(owner)[...].astype(F32)

                    self.out(owner)[...] = stage[...].astype(BF16)
                    copy_of(self.out(owner), slots(owner), self.send(owner), recv(owner), device).start()

        def total(self, stage):
            stage[...] = self.part(me)
            for slots, recv, device, _, joined in self.ways:
                @pl.when(joined)
                def _():
                    copy_of(slots(me), slots(me), self.send(me), recv(me), device).wait_recv()
                    stage[...] += slots(me)[...].astype(F32)

        def finish(self):
            for i in range(n_head):
                @pl.when(me != i)
                def _():
                    slot = self.out(i)
                    copy_of(slot, slot, self.send(i), self.send(i), right).wait_send()

    def query_part(c):
        def part(owner):
            at = pl.multiple_of(owner * q_cols, q_cols)
            return nn(wq[pl.ds(at, q_cols), :], gq_t[:, c * part_rows:(c + 1) * part_rows])

        return part

    def kv_part(owner):
        return gkv_own[pl.ds(pl.multiple_of(owner * kv_cols, 8), kv_cols), :]

    q_reduces = [
        Reduce(
            query_part(c),
            lambda i, c=c: rq_out.at[c, i],
            lambda i, c=c: rq_right.at[c, i],
            lambda i, c=c: rq_left.at[c, i],
            lambda i, c=c: rq_send.at[c, i],
            lambda i, c=c: rq_rr.at[c, i],
            lambda i, c=c: rq_rl.at[c, i],
            (stage_right, stage_left),
        )
        for c in range(chunks)
    ]
    kv_stage = (gkv_ref, gkv_ref)
    kv_reduce = Reduce(
        kv_part,
        lambda i: rkv_out.at[i],
        lambda i: rkv_right.at[i],
        lambda i: rkv_left.at[i],
        lambda i: rkv_send.at[i],
        lambda i: rkv_rr.at[i],
        lambda i: rkv_rl.at[i],
        kv_stage,
    )

    for c in range(chunks):
        hooks = []
        if c + 1 < chunks:
            hooks += [functools.partial(q_step, c + 1, t) for t in range(last)]
        if c > 0:
            hooks += [functools.partial(q_reduces[c - 1].step, t) for t in range(last)]
        attention(c, hooks)
        if c + 1 < chunks:
            for t in range(last):
                add_arrived(c + 1, t)
            finish_queries(c + 1)

    def project(row):
        return nt(wk[...], gk[row:row + rows, :]) + nt(wv[...], gv[row:row + rows, :])

    final = q_reduces[chunks - 1]
    if last > 0:
        final.step(0)
    back_out[:KVL, :] = project(0).astype(BF16)
    back_out[KVL:, :] = krope[:, :rows].astype(BF16)
    back = copy_of(back_out, back_in, b_send, b_recv, before)
    back.start()
    gkv_own[:KVL, :] = project(rows)
    gkv_own[KVL:, :] = krope[:, rows:]
    if last > 1:
        final.step(1)
    back.wait_recv()
    gkv_own[...] += back_in[...].astype(F32)
    for t in range(last):
        kv_reduce.step(t)
        if t + 2 < last:
            final.step(t + 2)

    for c in range(chunks):
        q_reduces[c].total(stage_right)
        gq_ref[:, c * part_rows:(c + 1) * part_rows] = stage_right[...]
    kv_reduce.total(gkv_ref)

    kv_gather.finish()
    kv_reduce.finish()
    for c in range(chunks):
        q_gathers[c].finish()
        q_reduces[c].finish()
    for i in range(n_head):
        copy_of(kv_ref, kv_prev.at[i], p_send.at[i], p_recv.at[i], after).wait_send()
    back.wait_send()


CHUNKS = 1
UNROLL = 2


def on_device(n_ctx, n_head, q_latent, kv_latent, w_query, w_key, w_value, d_out):
    rows, q_cols = q_latent.shape
    kv_cols = kv_latent.shape[1]
    ql, qw = w_query.shape
    kw = w_key.shape[1]
    kvw = n_head * kv_cols
    heads = kw // NOPE
    part_rows = rows // CHUNKS
    held = 2 * rows - part_rows if CHUNKS > 1 else 8
    vmem = pl.BlockSpec(memory_space=pltpu.VMEM)
    hbm = pl.BlockSpec(memory_space=pl.ANY)
    dma = pltpu.SemaphoreType.DMA
    some = (n_head,)
    each = (CHUNKS, n_head)
    out_t, gq_t, gkv_t = pl.pallas_call(
        functools.partial(kernel, n_ctx, n_head, CHUNKS),
        out_shape=(
            jax.ShapeDtypeStruct((kw, rows), BF16),
            jax.ShapeDtypeStruct((q_cols, rows), F32),
            jax.ShapeDtypeStruct((kv_cols, rows), F32),
        ),
        in_specs=[vmem, vmem, vmem, hbm, hbm, hbm],
        out_specs=(vmem, vmem, vmem),
        scratch_shapes=[
            pltpu.VMEM((ql, qw), BF16),
            pltpu.VMEM((KVL, kw), BF16),
            pltpu.VMEM((KVL, kw), BF16),
            pltpu.VMEM((kw, KVL), BF16),
            pltpu.VMEM((kw, KVL), BF16),
            pltpu.VMEM((kw, rows), BF16),
            pltpu.VMEM((CHUNKS, n_head, part_rows, q_cols), BF16),
            pltpu.VMEM((n_head, kv_cols, rows), BF16),
            pltpu.VMEM((n_head, kv_cols, rows), BF16),
            pltpu.VMEM((2 * rows, kvw), BF16),
            pltpu.VMEM((kvw, 2 * rows), BF16),
            pltpu.VMEM((rows, qw), F32),
            pltpu.VMEM((qw, rows), BF16),
            pltpu.VMEM((2 * rows, kw), BF16),
            pltpu.VMEM((kw, 2 * rows), BF16),
            pltpu.VMEM((2 * rows, kw), BF16),
            pltpu.VMEM((kw, 2 * rows), BF16),
            pltpu.VMEM((qw, rows), BF16),
            pltpu.VMEM((2 * rows, kw), BF16),
            pltpu.VMEM((2 * rows, kw), BF16),
            pltpu.VMEM((held, kw), F32),
            pltpu.VMEM((held, kw), F32),
            pltpu.VMEM((heads, ROPE, held), F32),
            pltpu.VMEM((ROPE, 2 * rows), F32),
            pltpu.VMEM((kvw, rows), BF16),
            pltpu.VMEM((kvw, rows), BF16),
            pltpu.VMEM((CHUNKS, n_head, q_cols, part_rows), BF16),
            pltpu.VMEM((CHUNKS, n_head, q_cols, part_rows), BF16),
            pltpu.VMEM((CHUNKS, n_head, q_cols, part_rows), BF16),
            pltpu.VMEM((n_head, kv_cols, rows), BF16),
            pltpu.VMEM((n_head, kv_cols, rows), BF16),
            pltpu.VMEM((n_head, kv_cols, rows), BF16),
            pltpu.VMEM((kvw, rows), F32),
            pltpu.VMEM((q_cols, part_rows), F32),
            pltpu.VMEM((q_cols, part_rows), F32),
            pltpu.VMEM((2 * rows, rows), F32),
            dma((3,)),
            dma(some), dma(some), dma(some),
            dma(each), dma(each), dma(each),
            dma(some), dma(some),
            dma, dma,
            dma(each), dma(each), dma(each),
            dma(some), dma(some), dma(some),
        ],
        compiler_params=pltpu.CompilerParams(
            collective_id=0, has_side_effects=True, vmem_limit_bytes=62 * 1024 * 1024,
        ),
        name="latent_attention",
    )(q_latent, kv_latent.T, d_out, w_query, w_key, w_value)
    return out_t.T, gq_t.T, gkv_t.T


def solution(mesh):
    return jax.shard_map(
        functools.partial(on_device, mesh.shape["ctx"], mesh.shape["head"]),
        mesh=mesh,
        in_specs=(
            P("ctx", "head"),
            P("ctx", "head"),
            P(None, "head"),
            P(None, "head"),
            P(None, "head"),
            P("ctx", "head"),
        ),
        out_specs=(P("ctx", "head"), P("ctx", "head"), P("ctx", "head")),
        check_vma=False,
    )
```

time: 92.6 us -> 80.5 us (0.87)
  Pallas kernels: 86.2 us -> 75.5 us
  local copies, waits for them, and re-layouts: 5.55 us -> 3.91 us
    pallas_call x1, Pallas kernels: 86.2 us -> 75.5 us  [on_device(): pl.pallas_call(functools.partial(kernel, n_ctx, n_head, CHUNKS), out_shap...]
    unnamed x8 -> x7, local copies, waits for them, and re-layouts: 5.55 us -> 3.91 us
where the time goes in v2:
time: 80.5 us; the launch traced here: 80.1 us
  Pallas kernels  75.5 us (94%)
  local copies, waits for them, and re-layouts  3.91 us (5%)
    pallas_call x1, Pallas kernels, on_device(): pl.pallas_call(functools.partial(kernel, n_ctx, n_head, CHUNKS), out_shap...  75.5 us
    unnamed x7, local copies, waits for them, and re-layouts  3.91 us

profile of v2, /device:TPU:0, one launch (start us, length us, event | category | flops | bytes accessed | tf_op | source)
XLA Modules:
  0.0 80.1 jit_solution(3705723458183220586)
XLA Ops:
  0.6 75.5 %latent_attention.1 = (bf16[2048,256]{1,0:T(8,128)(2,1)}, f32[384,256]{1,0:T(8,128)}, f32[144,256]{1,0:T(8,128)}) custom-call(bf16[256,384]{1,0:T(8,128)(2,1)} %q_ref.1, bf16[144,256]{1,0:T(8,128)(2,1)} %bitcast.7, bf16[256,2048]{1,0:T(8,128)(2,1)} %do_ref.1, bf16[1536,3072]{1,0:T(8,128)(2,1)} %wq_hbm.1, bf16[512,2048]{1,0:T(8,128)(2,1)} %wk_hbm.1, ...), custom_call_target="tpu_custom_call" | custom-call | tf_op jit(solution)/shard_map/latent_attention/pallas_call | solution.py:446
  76.2 0.0 copy-start
  76.2 0.0 copy-start.1
  76.2 2.3 %copy.9 = bf16[256,2048]{1,0:T(8,128)(2,1)} copy(bf16[256,2048]{0,1:T(8,128)(2,1)} %bitcast.4) | data formatting | bytes 2097152
  78.5 0.0 copy-done
  78.5 0.9 %copy.10 = f32[256,384]{1,0:T(8,128)} copy(f32[256,384]{0,1:T(8,128)S(1)} %bitcast.5) | data formatting | bytes 786432
  79.4 0.0 copy-done.1
  79.5 0.7 copy.12
Async XLA Ops:
  76.2 2.3 %copy-start = (f32[384,256]{1,0:T(8,128)S(1)}, f32[384,256]{1,0:T(8,128)}, u32[]{:S(2)}) copy-start(f32[384,256]{1,0:T(8,128)} %get-tuple-element.7) | copy-start | bytes 1179652
  76.2 3.3 %copy-start.1 = (f32[144,256]{1,0:T(8,128)S(1)}, f32[144,256]{1,0:T(8,128)}, u32[]{:S(2)}) copy-start(f32[144,256]{1,0:T(8,128)} %get-tuple-element.8) | copy-start | bytes 442372
